TPU v7x, 256 devices: a whole 4x4x8 slice. The times are simulated.
256 devices in a mesh: expert: 64 (over x, z, core), mp: 4 (over y).
Axes of the slice: x: 4, y: 4, z: 8, core: 2. Of those that a mesh axis runs over, the one named last changes fastest.
Arguments:
- tokens: bfloat16 [1536, 6144], P('expert', 'mp'), may hold values from -6 to 6
- mix_weights: float32 [1536, 2], P('expert'), may hold values from 0.2 to 1
- routes: int32 [1536, 2], P('expert'), may hold values from 0 to 7, as said below
- w_gate: bfloat16 [64, 6144, 1024], P('expert', None, 'mp'), may hold values from -0.078125 to 0.078125
- w_up: bfloat16 [64, 6144, 1024], P('expert', None, 'mp'), may hold values from -0.078125 to 0.078125
- w_down: bfloat16 [64, 1024, 6144], P('expert', 'mp'), may hold values from -0.0625 to 0.0625
Outputs:
- mixed_out: bfloat16 [1536, 6144], P('expert', 'mp')
Inputs may be any that keep to these rules, and one draw needn't show every extreme that they name: `routes`: each row names 2 different experts, and every expert is named by some row. Among the 24 rows of one index of the expert axis no expert is named more than 12 times, and on some indices one is named exactly 12 times.
All inputs are finite; a program needn't handle non-finite values.
Results may differ from a plain program's by a relative error of at most 0.011.
Values may be sent and summed in bfloat16 or wider, within the bound.
No kernel may reach another device: no remote copies, remote signals or barrier semaphores. Data moves between devices by JAX's collectives and lax.ppermute only.
A program may use at most 128 MiB of HBM per device.

v0:
```python
import jax
import jax.numpy as jnp
from jax import lax
from jax.sharding import Mesh
from jax.sharding import PartitionSpec as P

EXPERTS = 8
TOP = 2
EXPERT = ("expert_0", "expert_1", "expert_2")


def joined_along(pieces, dim):
    shape = list(pieces.shape[1:])
    shape[dim] *= pieces.shape[0]
    return jnp.moveaxis(pieces, 0, dim).reshape(shape)


def copy_for_each(value, axis):
    size = lax.axis_size(axis)
    return lax.all_to_all(
        jnp.broadcast_to(value[None], (size, *value.shape)), axis, 0, 0, tiled=True
    )


def collect(value, axis, dim):
    return joined_along(copy_for_each(value, axis), dim)


def split_up(value, dim, size):
    shape = value.shape
    pieces = value.reshape(*shape[:dim], size, shape[dim] // size, *shape[dim + 1 :])
    return jnp.moveaxis(pieces, dim, 0)


def exchange_in_order(pieces, axes, sequence):
    shape = [lax.axis_size(a) for a in axes]
    pieces = pieces.reshape(*shape, *pieces.shape[1:])
    for k in sequence:
        pieces = lax.all_to_all(pieces, axes[k], split_axis=k, concat_axis=k, tiled=True)
    return pieces.reshape(-1, *pieces.shape[len(axes) :])


def exchange_by_chip(value, groups, sequence, split_dim, concat_dim):
    size = lax.axis_size(groups[0]) * lax.axis_size(groups[1])
    pieces = split_up(value, split_dim, size)
    return joined_along(exchange_in_order(pieces, groups, sequence), concat_dim)


def pack_rows(pick_tokens, features, repeats):
    packed = jnp.einsum(
        "tem,tc->emc", pick_tokens, features, preferred_element_type=jnp.float32
    ).astype(jnp.bfloat16)
    spread = jnp.broadcast_to(packed[:, None], (packed.shape[0], repeats) + packed.shape[1:])
    return spread.reshape((packed.shape[0] * repeats,) + packed.shape[1:])


def activate(gate_act, up_act):
    return (jax.nn.silu(gate_act) * up_act).astype(jnp.bfloat16)


def local(tokens, mix_weights, routes, w_gate, w_up, w_down):
    tok_rows = tokens.shape[0]
    senders = lax.axis_size(EXPERT)
    group_size = senders // EXPERTS
    capacity = 5 * tok_rows * senders * TOP // (4 * EXPERTS)
    most_rows = tok_rows // 2
    labels = jnp.arange(EXPERTS, dtype=jnp.int32)
    flat_ids = routes.reshape(-1)
    marked = (flat_ids[:, None] == labels[None, :]).astype(jnp.int32)
    earlier = jnp.cumsum(marked, axis=0) - marked
    local_rank = jnp.sum(earlier * marked, axis=1)
    counts = jnp.sum(marked, axis=0)
    count_grid = collect(counts[None, :], EXPERT, 0)
    my_index = lax.axis_index(EXPERT)
    sender_ids = jnp.arange(senders, dtype=jnp.int32)
    lower_mask = (sender_ids[:, None] < my_index).astype(jnp.int32)
    offsets = jnp.sum(count_grid * lower_mask, axis=0)
    slot_ids = jnp.sum(marked * offsets[None, :], axis=1) + local_rank
    keep_mask = (slot_ids < capacity).astype(jnp.int32)
    rank_hit = (local_rank[:, None] == jnp.arange(most_rows, dtype=jnp.int32)[None, :]).astype(
        jnp.int32
    ) * keep_mask[:, None]
    assign_pick = marked[:, :, None] * rank_hit[:, None, :]
    pick_tokens = jnp.sum(assign_pick.reshape(tok_rows, TOP, EXPERTS, most_rows), axis=1).astype(
        jnp.bfloat16
    )
    weighted = assign_pick.astype(jnp.float32) * mix_weights.reshape(-1)[:, None, None]
    combine_w = jnp.sum(weighted.reshape(tok_rows, TOP, EXPERTS * most_rows), axis=1)
    gate_rows = w_gate[0]
    up_rows = w_up[0]
    down_rows = w_down[0]
    arrived = lax.all_to_all(
        pack_rows(pick_tokens, tokens, group_size), EXPERT, split_axis=0, concat_axis=0, tiled=True
    )
    arrived_rows = arrived.reshape(senders * most_rows, arrived.shape[2])
    my_expert = my_index // group_size
    column_counts = jnp.sum(count_grid * (labels[None, :] == my_expert).astype(jnp.int32), axis=1)
    starts = jnp.cumsum(column_counts) - column_counts
    slot_pos = jnp.arange(capacity, dtype=jnp.int32)
    slot_ends = starts + column_counts
    source_of = jnp.minimum(
        jnp.sum((slot_ends[None, :] <= slot_pos[:, None]).astype(jnp.int32), axis=1), senders - 1
    )
    source_hit = (sender_ids[None, :] == source_of[:, None]).astype(jnp.int32)
    start_of = jnp.sum(source_hit * starts[None, :], axis=1)
    slot_valid = slot_pos < jnp.sum(column_counts)
    fetch_idx = jnp.where(slot_valid, source_of * most_rows + slot_pos - start_of, 0)
    in_rows = jnp.where(
        slot_valid[:, None], jnp.take(arrived_rows, fetch_idx, axis=0), jnp.zeros((), jnp.bfloat16)
    )
    shard_piece = lax.all_gather(in_rows, "mp", axis=1, tiled=True)
    gate_act = jnp.dot(shard_piece, gate_rows, preferred_element_type=jnp.float32)
    up_act = jnp.dot(shard_piece, up_rows, preferred_element_type=jnp.float32)
    hidden = activate(gate_act, up_act)
    part_sum = jnp.dot(hidden, down_rows, preferred_element_type=jnp.float32)
    reduced = lax.psum_scatter(part_sum.astype(jnp.bfloat16), "mp", scatter_dimension=1, tiled=True)
    out_width = reduced.shape[1]
    buffer_pos = jnp.arange(most_rows, dtype=jnp.int32)
    slot_back = starts[:, None] + buffer_pos[None, :]
    back_valid = (buffer_pos[None, :] < column_counts[:, None]) & (slot_back < capacity)
    back_idx = jnp.where(back_valid, slot_back, 0).reshape(-1)
    back_rows = jnp.where(
        back_valid.reshape(-1)[:, None],
        jnp.take(reduced, back_idx, axis=0),
        jnp.zeros((), jnp.bfloat16),
    )
    returned = exchange_by_chip(
        back_rows.reshape(senders, most_rows, out_width),
        (("expert_0", "expert_1"), "expert_2"),
        (1, 0),
        0,
        0,
    )
    summed = jnp.sum(
        returned.reshape(EXPERTS, group_size, most_rows, out_width).astype(jnp.float32), axis=1
    )
    result = jnp.dot(
        combine_w, summed.reshape(EXPERTS * most_rows, out_width), precision=lax.Precision.HIGHEST
    )
    return result.astype(jnp.bfloat16)


def solution(mesh):
    torus = Mesh(
        mesh.devices.reshape(4, 8, 2, mesh.shape["mp"]), ("expert_0", "expert_1", "expert_2", "mp")
    )
    placed = (
        P(EXPERT, "mp"),
        P(EXPERT, None),
        P(EXPERT, None),
        P(EXPERT, None, "mp"),
        P(EXPERT, None, "mp"),
        P(EXPERT, "mp", None),
    )
    return jax.shard_map(
        local, mesh=torus, in_specs=placed, out_specs=P(EXPERT, "mp"), check_vma=False
    )
```

profile of v0, /device:TPU:6, one launch (start us, length us, event | category | flops | bytes accessed | tf_op | source)
XLA Modules:
  0.0 377.2 jit_solution(595688700204690243)
XLA Ops:
  6.5 0.9 copy.54
  7.4 0.1 eq.76
  7.5 0.1 fusion.15
  7.6 0.6 broadcast_in_dim.86
  8.3 12.2 %all-to-all-start = ((s32[64,1,8]{2,1,0:T(1,128)}), s32[64,1,8]{2,1,0:T(1,128)S(1)}, u32[]{:S(2)}, u32[]{:S(2)}) async-start(s32[64,1,8]{2,1,0:T(1,128)} %broadcast_in_dim.86), calls=%async_computation | async-start | bytes 65536 | tf_op jit(solution)/shard_map/all_to_all | solution.py:20
  20.5 0.1 fusion.13
  20.5 0.7 fusion.18
  21.2 0.1 reduce_window_sum.18
  21.3 6.7 %all-to-all-done = s32[64,1,8]{2,1,0:T(1,128)S(1)} async-done(((s32[64,1,8]{2,1,0:T(1,128)}), s32[64,1,8]{2,1,0:T(1,128)S(1)}, u32[]{:S(2)}, u32[]{:S(2)}) %all-to-all-start) | async-done | bytes 2080 | tf_op jit(solution)/shard_map/all_to_all | solution.py:20
  28.0 0.1 copy.55
  28.0 0.7 fusion.20
  28.8 0.2 select_reduce_fusion.2
  28.9 0.1 reduce_sum.119
  29.0 0.1 eq.91
  29.1 0.1 copy.58
  29.2 0.1 copy.59
  29.4 1.1 convolution_convert_fusion.1
  30.5 2.1 broadcast_in_dim.93
  32.6 7.5 %all-to-all-start.1 = ((bf16[64,12,1536]{2,1,0:T(8,128)(2,1)}), bf16[64,12,1536]{2,1,0:T(8,128)(2,1)}, u32[]{:S(2)}, u32[]{:S(2)}) async-start(bf16[64,12,1536]{2,1,0:T(8,128)(2,1)} %bitcast.37), calls=%async_computation.1 | async-start | bytes 6291456 | tf_op jit(solution)/shard_map/all_to_all | solution.py:92
  40.0 0.0 all-gather.2.cloned.1.call-start
  40.1 0.1 copy.57
  40.2 0.1 reduce-window.4
  40.3 0.1 reduce.3
  40.4 0.1 convert_reduce_fusion.1
  40.5 0.1 select_reduce_fusion
  40.6 0.7 compare_select_fusion.2
  41.3 0.7 iota_compare_fusion.7
  41.9 68.9 %all-to-all-done.1 = bf16[64,12,1536]{2,1,0:T(8,128)(2,1)} async-done(((bf16[64,12,1536]{2,1,0:T(8,128)(2,1)}), bf16[64,12,1536]{2,1,0:T(8,128)(2,1)}, u32[]{:S(2)}, u32[]{:S(2)}) %all-to-all-start.1) | async-done | bytes 2359328 | tf_op jit(solution)/shard_map/all_to_all | solution.py:92
  110.9 4.9 %reshape.343 = bf16[768,1536]{1,0:T(8,128)(2,1)} reshape(bf16[64,12,1536]{2,1,0:T(8,128)(2,1)} %all-to-all-done.1) | data formatting | bytes 4718592 | tf_op jit(solution)/shard_map/reshape | solution.py:95
  115.8 6.4 %gather_fusion = bf16[480,1536]{1,0:T(8,128)(2,1)} fusion(bf16[768,1536]{1,0:T(8,128)(2,1)} %reshape.343, s32[1024]{0:T(1024)S(1)} %pad_clamp_fusion.1), kind=kCustom, calls=%fused_computation | custom fusion | bytes 2951040 | tf_op jit(solution)/shard_map/jit(_take)/gather | solution.py:109
  122.1 2.8 select_select_fusion.1
  124.9 0.0 all-gather.2.cloned.1.call-update
  124.9 0.2 reduce-scatter.2.cloned.1.call-start
  125.1 63.9 %all-gather.2.cloned.1.call-done = bf16[480,6144]{1,0:T(8,128)(2,1)} async-done(((bf16[480,1536]{1,0:T(8,128)(2,1)}), bf16[480,6144]{1,0:T(8,128)(2,1)}) %all-gather.2.cloned.1.call-update) | async-done | bytes 5898256 | tf_op jit(solution)/shard_map/all_gather | solution.py:111
  189.1 5.4 %fusion.3 = f32[480,256]{1,0:T(8,128)S(1)} fusion(bf16[480,6144]{1,0:T(8,128)(2,1)} %all-gather.2.cloned.1.call-done, bf16[1,6144,256]{2,1,0:T(8,128)(2,1)} %param.9), kind=kOutput, calls=%fused_computation.8 | convolution fusion | flops 1509949440 | bytes 9535488 | tf_op jit(solution)/shard_map/dot_general | solution.py:112
  194.5 0.8 copy-done.3
  195.3 1.7 fusion.8
  197.0 4.2 %convolution_convert_fusion = bf16[480,6144]{1,0:T(8,128)(2,1)} fusion(bf16[480,256]{1,0:T(8,128)(2,1)S(1)} %fusion.8, bf16[1,256,6144]{2,1,0:T(8,128)(2,1)S(1)} %copy-done), kind=kOutput, calls=%fused_computation.2 | convolution fusion | flops 1512898560 | bytes 9289728 | tf_op jit(solution)/shard_map/dot_general | solution.py:115
  201.2 0.0 reduce-scatter.2.cloned.1.call-update
  201.3 0.1 reshape.340
  201.4 0.1 lt.154
  201.5 0.1 iota_add_fusion
  201.5 0.1 add.125
  201.7 0.1 iota_compare_fusion.2
  201.7 0.1 lt.172
  201.9 0.2 compare_and_fusion.1
  202.1 63.3 %reduce-scatter.2.cloned.1.call-done = bf16[480,1536]{1,0:T(8,128)(2,1)} async-done(((bf16[480,6144]{1,0:T(8,128)(2,1)}), bf16[480,1536]{1,0:T(8,128)(2,1)}) %reduce-scatter.2.cloned.1.call-update) | async-done | bytes 1474576 | tf_op jit(solution)/shard_map/reduce_scatter | solution.py:116
  265.4 7.5 %gather_fusion.1 = bf16[768,1536]{1,0:T(8,128)(2,1)} fusion(bf16[480,1536]{1,0:T(8,128)(2,1)} %reduce-scatter.2.cloned.1.call-done, s32[1024]{0:T(1024)S(1)} %pad_clamp_fusion), kind=kCustom, calls=%fused_computation.1 | custom fusion | bytes 4721664 | tf_op jit(solution)/shard_map/jit(_take)/gather | solution.py:124
  272.8 4.8 %gather.12 = bf16[32,2,1,12,1536]{4,3,1,0,2:T(8,128)(2,1)} reshape(bf16[768,1536]{1,0:T(8,128)(2,1)} %gather_fusion.1) | data formatting | bytes 4718592 | tf_op jit(solution)/shard_map/jit(_take)/gather | solution.py:124
  277.6 2.2 select_select_fusion
  279.8 1.3 copy.61
  281.1 5.6 %all_to_all.20 = bf16[32,2,1,12,1536]{4,0,3,2,1:T(8,128)(2,1)S(1)} all-to-all(bf16[32,2,1,12,1536]{4,0,3,2,1:T(8,128)(2,1)S(1)} %copy.61), channel_id=1, replica_groups=mesh['expert_0'=4,'expert_1'=8,'expert_2'=2,'mp'=4] {'expert_2'}, dimensions={1} | all-to-all | bytes 4718592 | tf_op jit(solution)/shard_map/all_to_all | solution.py:39
  286.7 3.8 %copy.62 = bf16[32,2,1,12,1536]{4,1,3,2,0:T(2,128)(2,1)} copy(bf16[32,2,1,12,1536]{4,0,3,2,1:T(8,128)(2,1)S(1)} %all_to_all.20) | data formatting | bytes 4718592 | tf_op jit(solution)/shard_map/all_to_all | solution.py:39
  290.5 10.4 %all-to-all-start.3 = ((bf16[32,2,1,12,1536]{4,1,3,2,0:T(2,128)(2,1)}), bf16[32,2,1,12,1536]{4,1,3,2,0:T(2,128)(2,1)}, u32[]{:S(2)}, u32[]{:S(2)}) async-start(bf16[32,2,1,12,1536]{4,1,3,2,0:T(2,128)(2,1)} %copy.62), calls=%async_computation.4 | async-start | bytes 4718592 | tf_op jit(solution)/shard_map/all_to_all | solution.py:39
  300.9 0.1 copy.56
  301.0 0.1 fusion.14
  301.1 0.1 multiply_convert_fusion
  301.2 0.1 convert_element_type.71
  301.3 0.1 multiply_reduce_fusion.1
  301.4 55.5 %all-to-all-done.3 = bf16[32,2,1,12,1536]{4,1,3,2,0:T(2,128)(2,1)} async-done(((bf16[32,2,1,12,1536]{4,1,3,2,0:T(2,128)(2,1)}), bf16[32,2,1,12,1536]{4,1,3,2,0:T(2,128)(2,1)}, u32[]{:S(2)}, u32[]{:S(2)}) %all-to-all-start.3) | async-done | bytes 2359328 | tf_op jit(solution)/shard_map/all_to_all | solution.py:39
  356.9 8.2 %convert_reduce_fusion = f32[32,12,1536]{2,1,0:T(8,128)S(1)} fusion(bf16[32,2,1,12,1536]{4,1,3,2,0:T(2,128)(2,1)} %all-to-all-done.3), kind=kLoop, calls=%fused_computation.3 | loop fusion | flops 1769472 | bytes 4718592 | tf_op jit(solution)/shard_map/reduce_sum | solution.py:134
  365.1 1.1 bitcast_reduce_fusion
  366.3 2.0 reshape.344
  368.3 2.1 convolution_convert_fusion.2
  (20 shorter events, 0.1 us)
Async XLA Ops:
  6.5 190.5 %copy-start = (bf16[1,256,6144]{2,1,0:T(8,128)(2,1)S(1)}, bf16[1,256,6144]{2,1,0:T(8,128)(2,1)}, u32[]{:S(2)}) copy-start(bf16[1,256,6144]{2,1,0:T(8,128)(2,1)} %param.11) | copy-start | bytes 9437188
  8.3 19.7 %all-to-all-start = ((s32[64,1,8]{2,1,0:T(1,128)}), s32[64,1,8]{2,1,0:T(1,128)S(1)}, u32[]{:S(2)}, u32[]{:S(2)}) async-start(s32[64,1,8]{2,1,0:T(1,128)} %broadcast_in_dim.86), calls=%async_computation | async-start | bytes 65536 | tf_op jit(solution)/shard_map/all_to_all | solution.py:20
  32.6 78.3 %all-to-all-start.1 = ((bf16[64,12,1536]{2,1,0:T(8,128)(2,1)}), bf16[64,12,1536]{2,1,0:T(8,128)(2,1)}, u32[]{:S(2)}, u32[]{:S(2)}) async-start(bf16[64,12,1536]{2,1,0:T(8,128)(2,1)} %bitcast.37), calls=%async_computation.1 | async-start | bytes 6291456 | tf_op jit(solution)/shard_map/all_to_all | solution.py:92
  40.0 149.1 %all-gather.2.cloned.1.call-start = ((), (), s32[]{:S(2)}) async-start(), calls=%async_computation.5 | async-start | bytes 7372800 | tf_op jit(solution)/shard_map/all_gather | solution.py:111
  124.9 140.4 %reduce-scatter.2.cloned.1.call-start = ((), (), s32[]{:S(2)}) async-start(), calls=%async_computation.6 | async-start | bytes 7372800 | tf_op jit(solution)/shard_map/reduce_scatter | solution.py:116
  189.1 5.5 %copy-start.2 = (bf16[480,6144]{1,0:T(8,128)(2,1)S(1)}, bf16[480,6144]{1,0:T(8,128)(2,1)}, u32[]{:S(2)}) copy-start(bf16[480,6144]{1,0:T(8,128)(2,1)} %all-gather.2.cloned.1.call-done) | copy-start | bytes 17694724
  189.1 6.2 %copy-start.3 = (bf16[1,6144,256]{2,1,0:T(8,128)(2,1)S(1)}, bf16[1,6144,256]{2,1,0:T(8,128)(2,1)}, u32[]{:S(2)}) copy-start(bf16[1,6144,256]{2,1,0:T(8,128)(2,1)} %param.10) | copy-start | bytes 9437188
  290.5 10.4 %copy-start.1 = (f32[24,2]{0,1:T(2,128)S(1)}, f32[24,2]{0,1:T(2,128)}, u32[]{:S(2)}) copy-start(f32[24,2]{0,1:T(2,128)} %param.7) | copy-start | bytes 580
  290.5 66.4 %all-to-all-start.3 = ((bf16[32,2,1,12,1536]{4,1,3,2,0:T(2,128)(2,1)}), bf16[32,2,1,12,1536]{4,1,3,2,0:T(2,128)(2,1)}, u32[]{:S(2)}, u32[]{:S(2)}) async-start(bf16[32,2,1,12,1536]{4,1,3,2,0:T(2,128)(2,1)} %copy.62), calls=%async_computation.4 | async-start | bytes 4718592 | tf_op jit(solution)/shard_map/all_to_all | solution.py:39
Sparse Core Ops, SparseCore 0:
  125.0 63.9 all-gather.1
  201.4 63.9 reduce-scatter.1
where the time goes:
time: 378 us; the launch traced here: 377 us
  waiting for transfers between devices  258 us (68%)
  local copies, waits for them, and re-layouts  36.2 us (10%)
  starting transfers between devices  30.2 us (8%)
  other arithmetic  18.5 us (5%)
  matrix products  14.6 us (4%)
  between operations  13.7 us (4%)
  blocking collectives  5.63 us (1%)
    all_to_all x1, waiting for transfers between devices, local(): lax.all_to_all(pack_rows(pick_tokens, tokens, group_size), EXPERT, split_...  68.9 us
    all_gather x1, waiting for transfers between devices, local(): shard_piece = lax.all_gather(in_rows, 'mp', axis=1, tiled=True)  63.9 us
    reduce_scatter x1, waiting for transfers between devices, local(): lax.psum_scatter(part_sum.astype(jnp.bfloat16), 'mp', scatter_dimension=1...  63.3 us
    all_to_all x1, waiting for transfers between devices, exchange_in_order(): lax.all_to_all(pieces, axes[k], split_axis=k, concat_axis=k, tiled=True)  55.5 us
    gather x2, local copies, waits for them, and re-layouts, local(): jnp.take(reduced, back_idx, axis=0)  12.2 us
    all_to_all x1, starting transfers between devices, copy_for_each(): lax.all_to_all(jnp.broadcast_to(value[None], (size, *value.shape)), axis,...  12.2 us
    all_to_all x1, starting transfers between devices, exchange_in_order(): lax.all_to_all(pieces, axes[k], split_axis=k, concat_axis=k, tiled=True)  10.4 us
    reduce_sum x2, other arithmetic, local(): jnp.sum(returned.reshape(EXPERTS, group_size, most_rows, out_width).astyp...  9.32 us
  transfers between devices with their start and end apart: 5, of which 5 were waited for; matrix products, arithmetic and copies ran while one was open for 1% of the time, Pallas kernels for 0%

commit v1 on v0

--- a/solution.py
+++ b/solution.py
@@ -108,7 +108,8 @@
     in_rows = jnp.where(
         slot_valid[:, None], jnp.take(arrived_rows, fetch_idx, axis=0), jnp.zeros((), jnp.bfloat16)
     )
-    shard_piece = lax.all_gather(in_rows, "mp", axis=1, tiled=True)
+    stack = jnp.stack([in_rows] * lax.axis_size("mp"))
+    shard_piece = jnp.concatenate(lax.all_to_all(stack, "mp", 0, 0), axis=1)
     gate_act = jnp.dot(shard_piece, gate_rows, preferred_element_type=jnp.float32)
     up_act = jnp.dot(shard_piece, up_rows, preferred_element_type=jnp.float32)
     hidden = activate(gate_act, up_act)

time: 378 us -> 376 us (level)
  blocking collectives: 5.63 us -> 77 us
  waiting for transfers between devices: 258 us -> 191 us
  matrix products: 14.6 us -> 10.8 us
    all_to_all x0 -> x1, blocking collectives: none -> 71.4 us  [local(): shard_piece = jnp.concatenate(lax.all_to_all(stack, 'mp', 0, 0), axis=1)]
    all_gather x1 -> x0, waiting for transfers between devices: 63.9 us -> none  [local(): shard_piece = lax.all_gather(in_rows, 'mp', axis=1, tiled=True)]
  transfers between devices with their start and end apart: 5 -> 4, of which waited for: 5 -> 4; matrix products, arithmetic and copies ran while one was open for 1% -> 1% of each run, Pallas kernels for 0% -> 0%
where the time goes in v1:
time: 376 us; the launch traced here: 375 us
  waiting for transfers between devices  191 us (51%)
  blocking collectives  77 us (20%)
  local copies, waits for them, and re-layouts  36.6 us (10%)
  starting transfers between devices  30 us (8%)
  other arithmetic  15.9 us (4%)
  between operations  13.7 us (4%)
  matrix products  10.8 us (3%)
    all_to_all x1, blocking collectives, local(): shard_piece = jnp.concatenate(lax.all_to_all(stack, 'mp', 0, 0), axis=1)  71.4 us
    all_to_all x1, waiting for transfers between devices, local(): lax.all_to_all(pack_rows(pick_tokens, tokens, group_size), EXPERT, split_...  68.9 us
    reduce_scatter x1, waiting for transfers between devices, local(): lax.psum_scatter(part_sum.astype(jnp.bfloat16), 'mp', scatter_dimension=1...  59.6 us
    all_to_all x1, waiting for transfers between devices, exchange_in_order(): lax.all_to_all(pieces, axes[k], split_axis=k, concat_axis=k, tiled=True)  55.5 us
    all_to_all x1, starting transfers between devices, copy_for_each(): lax.all_to_all(jnp.broadcast_to(value[None], (size, *value.shape)), axis,...  12.2 us
    gather x2, local copies, waits for them, and re-layouts, local(): jnp.take(reduced, back_idx, axis=0)  10.9 us
    all_to_all x1, starting transfers between devices, exchange_in_order(): lax.all_to_all(pieces, axes[k], split_axis=k, concat_axis=k, tiled=True)  10.4 us
    reduce_sum x2, other arithmetic, local(): jnp.sum(returned.reshape(EXPERTS, group_size, most_rows, out_width).astyp...  9.47 us
  transfers between devices with their start and end apart: 4, of which 4 were waited for; matrix products, arithmetic and copies ran while one was open for 1% of the time, Pallas kernels for 0%

profile of v1, /device:TPU:6, one launch (start us, length us, event | category | flops | bytes accessed | tf_op | source)
XLA Modules:
  0.0 374.9 jit_solution(11583925319145002250)
XLA Ops:
  6.5 0.9 copy.58
  7.4 0.1 eq.76
  7.5 0.1 fusion.15
  7.6 0.6 broadcast_in_dim.86
  8.3 12.2 %all-to-all-start = ((s32[64,1,8]{2,1,0:T(1,128)}), s32[64,1,8]{2,1,0:T(1,128)S(1)}, u32[]{:S(2)}, u32[]{:S(2)}) async-start(s32[64,1,8]{2,1,0:T(1,128)} %broadcast_in_dim.86), calls=%async_computation | async-start | bytes 65536 | tf_op jit(solution)/shard_map/all_to_all | solution.py:20
  20.5 0.1 fusion.13
  20.5 0.7 fusion.18
  21.2 0.1 reduce_window_sum.18
  21.3 6.7 %all-to-all-done = s32[64,1,8]{2,1,0:T(1,128)S(1)} async-done(((s32[64,1,8]{2,1,0:T(1,128)}), s32[64,1,8]{2,1,0:T(1,128)S(1)}, u32[]{:S(2)}, u32[]{:S(2)}) %all-to-all-start) | async-done | bytes 2080 | tf_op jit(solution)/shard_map/all_to_all | solution.py:20
  28.0 0.1 copy.59
  28.0 0.7 fusion.20
  28.8 0.2 select_reduce_fusion.2
  28.9 0.1 reduce_sum.119
  29.0 0.1 eq.91
  29.1 0.1 copy.62
  29.2 0.1 copy.63
  29.4 1.1 convolution_convert_fusion.1
  30.5 2.1 broadcast_in_dim.93
  32.6 7.5 %all-to-all-start.1 = ((bf16[64,12,1536]{2,1,0:T(8,128)(2,1)}), bf16[64,12,1536]{2,1,0:T(8,128)(2,1)}, u32[]{:S(2)}, u32[]{:S(2)}) async-start(bf16[64,12,1536]{2,1,0:T(8,128)(2,1)} %bitcast.41), calls=%async_computation.1 | async-start | bytes 6291456 | tf_op jit(solution)/shard_map/all_to_all | solution.py:92
  40.0 0.0 reduce-scatter.2.cloned.1.call-start
  40.1 0.1 copy.61
  40.2 0.1 reduce-window.4
  40.3 0.1 reduce.3
  40.4 0.1 convert_reduce_fusion.1
  40.5 0.1 select_reduce_fusion
  40.6 0.7 compare_select_fusion.2
  41.3 0.7 iota_compare_fusion.7
  41.9 68.9 %all-to-all-done.1 = bf16[64,12,1536]{2,1,0:T(8,128)(2,1)} async-done(((bf16[64,12,1536]{2,1,0:T(8,128)(2,1)}), bf16[64,12,1536]{2,1,0:T(8,128)(2,1)}, u32[]{:S(2)}, u32[]{:S(2)}) %all-to-all-start.1) | async-done | bytes 2359328 | tf_op jit(solution)/shard_map/all_to_all | solution.py:92
  110.9 4.9 %reshape.362 = bf16[768,1536]{1,0:T(8,128)(2,1)} reshape(bf16[64,12,1536]{2,1,0:T(8,128)(2,1)} %all-to-all-done.1) | data formatting | bytes 4718592 | tf_op jit(solution)/shard_map/reshape | solution.py:95
  115.8 6.3 %gather_fusion = bf16[480,1536]{1,0:T(8,128)(2,1)} fusion(bf16[768,1536]{1,0:T(8,128)(2,1)} %reshape.362, s32[1024]{0:T(1024)S(1)} %pad_clamp_fusion.1), kind=kCustom, calls=%fused_computation | custom fusion | bytes 2951040 | tf_op jit(solution)/shard_map/jit(_take)/gather | solution.py:109
  122.1 1.6 select_select_fusion.1
  123.7 0.5 stack.2
  124.2 71.4 %all_to_all.25 = bf16[4,480,1536]{2,1,0:T(8,128)(2,1)S(1)} all-to-all(bf16[4,480,1536]{2,1,0:T(8,128)(2,1)S(1)} %stack.2), channel_id=1, replica_groups=mesh['expert_0'=4,'expert_1'=8,'expert_2'=2,'mp'=4] {'mp'}, dimensions={0} | all-to-all | bytes 11796480 | tf_op jit(solution)/shard_map/all_to_all | solution.py:112
  195.6 0.8 copy.74
  196.5 1.0 copy-done.3
  197.5 1.7 fusion.3
  199.2 0.2 copy-done.4
  199.4 1.7 fusion.8
  201.1 4.2 %convolution_convert_fusion = bf16[480,6144]{1,0:T(8,128)(2,1)} fusion(bf16[480,256]{1,0:T(8,128)(2,1)S(1)} %fusion.8, bf16[1,256,6144]{2,1,0:T(8,128)(2,1)S(1)} %copy-done), kind=kOutput, calls=%fused_computation.2 | convolution fusion | flops 1512898560 | bytes 9289728 | tf_op jit(solution)/shard_map/dot_general | solution.py:116
  205.3 0.1 reshape.359
  205.4 0.1 lt.154
  205.6 0.1 iota_add_fusion
  205.6 0.1 add.125
  205.7 0.1 iota_compare_fusion.2
  205.8 0.1 lt.172
  206.0 0.2 compare_and_fusion.1
  206.2 59.6 %reduce-scatter.2.cloned.1.call-done = bf16[480,1536]{1,0:T(8,128)(2,1)} async-done(((bf16[480,6144]{1,0:T(8,128)(2,1)}), bf16[480,1536]{1,0:T(8,128)(2,1)}) %reduce-scatter.2.cloned.1.call-update) | async-done | bytes 1474576 | tf_op jit(solution)/shard_map/reduce_scatter | solution.py:117
  265.8 7.5 %gather_fusion.1 = bf16[768,1536]{1,0:T(8,128)(2,1)} fusion(bf16[480,1536]{1,0:T(8,128)(2,1)} %reduce-scatter.2.cloned.1.call-done, s32[1024]{0:T(1024)S(1)} %pad_clamp_fusion), kind=kCustom, calls=%fused_computation.1 | custom fusion | bytes 4721664 | tf_op jit(solution)/shard_map/jit(_take)/gather | solution.py:125
  273.3 3.4 gather.12
  276.7 0.6 select_select_fusion
  277.2 1.3 copy.66
  278.5 5.6 %all_to_all.26 = bf16[32,2,1,12,1536]{4,0,3,2,1:T(8,128)(2,1)S(1)} all-to-all(bf16[32,2,1,12,1536]{4,0,3,2,1:T(8,128)(2,1)S(1)} %copy.66), channel_id=1, replica_groups=mesh['expert_0'=4,'expert_1'=8,'expert_2'=2,'mp'=4] {'expert_2'}, dimensions={1} | all-to-all | bytes 4718592 | tf_op jit(solution)/shard_map/all_to_all | solution.py:39
  284.2 3.8 %copy.67 = bf16[32,2,1,12,1536]{4,1,3,2,0:T(2,128)(2,1)} copy(bf16[32,2,1,12,1536]{4,0,3,2,1:T(8,128)(2,1)S(1)} %all_to_all.26) | data formatting | bytes 4718592 | tf_op jit(solution)/shard_map/all_to_all | solution.py:39
  288.0 10.4 %all-to-all-start.4 = ((bf16[32,2,1,12,1536]{4,1,3,2,0:T(2,128)(2,1)}), bf16[32,2,1,12,1536]{4,1,3,2,0:T(2,128)(2,1)}, u32[]{:S(2)}, u32[]{:S(2)}) async-start(bf16[32,2,1,12,1536]{4,1,3,2,0:T(2,128)(2,1)} %copy.67), calls=%async_computation.5 | async-start | bytes 4718592 | tf_op jit(solution)/shard_map/all_to_all | solution.py:39
  298.4 0.1 copy.60
  298.5 0.1 fusion.14
  298.5 0.1 multiply_convert_fusion
  298.7 0.1 convert_element_type.71
  298.8 0.1 multiply_reduce_fusion.1
  298.9 55.5 %all-to-all-done.4 = bf16[32,2,1,12,1536]{4,1,3,2,0:T(2,128)(2,1)} async-done(((bf16[32,2,1,12,1536]{4,1,3,2,0:T(2,128)(2,1)}), bf16[32,2,1,12,1536]{4,1,3,2,0:T(2,128)(2,1)}, u32[]{:S(2)}, u32[]{:S(2)}) %all-to-all-start.4) | async-done | bytes 2359328 | tf_op jit(solution)/shard_map/all_to_all | solution.py:39
  354.4 8.3 %convert_reduce_fusion = f32[32,12,1536]{2,1,0:T(8,128)S(1)} fusion(bf16[32,2,1,12,1536]{4,1,3,2,0:T(2,128)(2,1)} %all-to-all-done.4), kind=kLoop, calls=%fused_computation.3 | loop fusion | flops 1769472 | bytes 4718592 | tf_op jit(solution)/shard_map/reduce_sum | solution.py:135
  362.8 1.1 bitcast_reduce_fusion
  363.9 2.0 reshape.365
  365.9 2.1 convolution_convert_fusion.2
  (22 shorter events, 0.1 us)
Async XLA Ops:
  6.5 194.6 %copy-start = (bf16[1,256,6144]{2,1,0:T(8,128)(2,1)S(1)}, bf16[1,256,6144]{2,1,0:T(8,128)(2,1)}, u32[]{:S(2)}) copy-start(bf16[1,256,6144]{2,1,0:T(8,128)(2,1)} %param.11) | copy-start | bytes 9437188
  8.3 19.7 %all-to-all-start = ((s32[64,1,8]{2,1,0:T(1,128)}), s32[64,1,8]{2,1,0:T(1,128)S(1)}, u32[]{:S(2)}, u32[]{:S(2)}) async-start(s32[64,1,8]{2,1,0:T(1,128)} %broadcast_in_dim.86), calls=%async_computation | async-start | bytes 65536 | tf_op jit(solution)/shard_map/all_to_all | solution.py:20
  32.6 78.3 %all-to-all-start.1 = ((bf16[64,12,1536]{2,1,0:T(8,128)(2,1)}), bf16[64,12,1536]{2,1,0:T(8,128)(2,1)}, u32[]{:S(2)}, u32[]{:S(2)}) async-start(bf16[64,12,1536]{2,1,0:T(8,128)(2,1)} %bitcast.41), calls=%async_computation.1 | async-start | bytes 6291456 | tf_op jit(solution)/shard_map/all_to_all | solution.py:92
  40.0 225.8 %reduce-scatter.2.cloned.1.call-start = ((), (), s32[]{:S(2)}) async-start(), calls=%async_computation.6 | async-start | bytes 7372800 | tf_op jit(solution)/shard_map/reduce_scatter | solution.py:117
  195.6 1.9 copy-start.3
  197.5 1.9 copy-start.4
  288.0 10.4 %copy-start.2 = (f32[24,2]{0,1:T(2,128)S(1)}, f32[24,2]{0,1:T(2,128)}, u32[]{:S(2)}) copy-start(f32[24,2]{0,1:T(2,128)} %param.7) | copy-start | bytes 580
  288.0 66.4 %all-to-all-start.4 = ((bf16[32,2,1,12,1536]{4,1,3,2,0:T(2,128)(2,1)}), bf16[32,2,1,12,1536]{4,1,3,2,0:T(2,128)(2,1)}, u32[]{:S(2)}, u32[]{:S(2)}) async-start(bf16[32,2,1,12,1536]{4,1,3,2,0:T(2,128)(2,1)} %copy.67), calls=%async_computation.5 | async-start | bytes 4718592 | tf_op jit(solution)/shard_map/all_to_all | solution.py:39
  354.4 13.6 %copy-start.1 = (bf16[1,256,6144]{2,1,0:T(8,128)(2,1)S(1)}, bf16[1,256,6144]{2,1,0:T(8,128)(2,1)}, u32[]{:S(2)}) copy-start(bf16[1,256,6144]{2,1,0:T(8,128)(2,1)} %param.11) | copy-start | bytes 9437188
Sparse Core Ops, SparseCore 0:
  205.5 60.2 reduce-scatter.1
